TPU v7x, 32 devices: a whole 2x2x4 slice. The times are simulated.
32 devices in a mesh: aa: 4 (over z), ba: 8 (over y, x, core).
Axes of the slice: x: 2, y: 2, z: 4, core: 2. Of those that a mesh axis runs over, the one named last changes fastest.
Arguments:
- grad_out: bfloat16 [4096, 4096], P('aa', 'ba')
- saved_input: bfloat16 [4096, 4096], P(('aa', 'ba'))
- keep_bits: int32 [4096, 128], P(('aa', 'ba')), may hold values from -2147483648 to 2147483647, as said below
- gain: float32 [4096], replicated, may hold values from 0.5 to 1.5
Outputs:
- grad_in: bfloat16 [4096, 4096], P(('aa', 'ba'))
- gain_grad: float32 [4096], P('ba')
Inputs may be any that keep to these rules, and one draw needn't show every extreme that they name: `keep_bits`: bit k of word w in row t (bit 31 being the sign bit) is the keep flag of feature 32 * w + k of token t; about nine in ten flags are 1.
All inputs are finite; a program needn't handle non-finite values.
Results may differ from a plain program's by a relative error of at most 0.001.
Values may be sent and summed in bfloat16 or wider, within the bound.
A program may use at most 64 MiB of HBM per device.

v0:
```python
import math
import jax
import jax.numpy as jnp
from jax import lax
from jax.sharding import PartitionSpec as P

KEEP_RATE = 0.9
EPSILON = 1e-06


def unpack_bits(words):
    shifts = jnp.arange(32, dtype=jnp.int32)
    bits = jnp.right_shift(words[:, :, None], shifts[None, None, :]) & 1
    return bits.reshape(words.shape[0], words.shape[1] * 32).astype(jnp.float32)


def rows_backward(grad_rows, input_rows, word_rows, gain):
    keep = unpack_bits(word_rows)
    dropped = input_rows.astype(jnp.float32) * keep * (1.0 / KEEP_RATE)
    inverse = lax.rsqrt(jnp.mean(dropped * dropped, axis=-1, keepdims=True) + EPSILON)
    normed = dropped * inverse
    grads = grad_rows.astype(jnp.float32)
    scaled = gain[None, :] * grads
    centre = jnp.mean(scaled * normed, axis=-1, keepdims=True)
    grad_in = (inverse * (scaled - normed * centre) * keep * (1.0 / KEEP_RATE)).astype(jnp.bfloat16)
    partial_sum = jnp.sum(grads * normed, axis=0)
    return (grad_in, partial_sum)


def per_device(grad_out, saved_input, keep_bits, gain):
    groups = lax.axis_size("ba")
    rows = grad_out.shape[0] // groups
    pieces = grad_out.reshape(groups, rows, grad_out.shape[1])
    arrived = lax.all_to_all(pieces, "ba", split_axis=0, concat_axis=2, tiled=True)
    grad_rows = arrived.reshape(rows, arrived.shape[2])
    grad_in, partial_sum = rows_backward(grad_rows, saved_input, keep_bits, gain)
    total_tokens = rows * groups * lax.axis_size("aa")
    owned = lax.psum_scatter(partial_sum, "ba", scatter_dimension=0, tiled=True)
    share = lax.psum(owned, "aa")
    gain_grad = share * (1.0 / math.sqrt(total_tokens))
    return (grad_in, gain_grad)


def solution(mesh):
    placed = (P("aa", "ba"), P(("aa", "ba"), None), P(("aa", "ba"), None), P())
    return jax.shard_map(
        per_device,
        mesh=mesh,
        in_specs=placed,
        out_specs=(P(("aa", "ba"), None), P("ba")),
        check_vma=False,
    )
```

profile of v0, /device:TPU:0, one launch (start us, length us, event | category | flops | bytes accessed | tf_op | source)
XLA Modules:
  0.0 63.3 jit_solution(16669645412910738614)
XLA Ops:
  0.6 2.3 %copy.13 = bf16[8,128,512]{1,2,0:T(8,128)(2,1)} copy(bf16[8,128,512]{2,1,0:T(8,128)(2,1)} %bitcast.48) | data formatting | bytes 2097152 | tf_op jit(solution)/shard_map/reshape | solution.py:33
  2.9 0.0 copy-start
  2.9 5.3 %all-to-all-start = ((bf16[8,128,512]{1,2,0:T(8,128)(2,1)}), bf16[8,128,512]{1,2,0:T(8,128)(2,1)S(1)}, u32[]{:S(2)}, u32[]{:S(2)}) async-start(bf16[8,128,512]{1,2,0:T(8,128)(2,1)} %copy.13), calls=%async_computation | async-start | bytes 2097152 | tf_op jit(solution)/shard_map/all_to_all | solution.py:34
  8.2 0.0 copy-done
  8.2 0.0 copy-start.2
  8.2 0.0 copy-start.3
  8.3 0.7 %copy.11 = bf16[128,4096]{0,1:T(8,128)(2,1)S(1)} copy(bf16[128,4096]{1,0:T(8,128)(2,1)S(1)} %copy-done) | data formatting | bytes 2097152 | tf_op args[1]
  8.9 0.0 copy-start.1
  9.0 0.1 shift_right_arithmetic.23
  9.0 0.0 copy-done.2
  9.1 0.1 copy.12
  9.2 0.0 copy-done.3
  9.2 0.6 dynamic-slice
  10.4 0.7 %multiply_reduce_fusion = f32[128]{0:T(128)S(1)} fusion(bf16[128,4096]{0,1:T(8,128)(2,1)S(1)} %copy.11, s32[4096]{0:T(1024)S(1)} %shift_right_arithmetic.23, s32[128,128]{0,1:T(8,128)S(1)} %copy.12), kind=kLoop, calls=%fused_computation.14 | loop fusion | flops 4194176 | bytes 1131008 | tf_op jit(solution)/shard_map/reduce_sum | solution.py:20
  11.2 12.4 %all-to-all-done = bf16[8,128,512]{1,2,0:T(8,128)(2,1)S(1)} async-done(((bf16[8,128,512]{1,2,0:T(8,128)(2,1)}), bf16[8,128,512]{1,2,0:T(8,128)(2,1)S(1)}, u32[]{:S(2)}, u32[]{:S(2)}) %all-to-all-start) | async-done | bytes 1048608 | tf_op jit(solution)/shard_map/all_to_all | solution.py:34
  23.6 0.0 copy-done.1
  23.6 2.0 %fusion.7 = (f32[4096]{0:T(1024)S(1)}, f32[128]{0:T(128)S(1)}) fusion(bf16[128,4096]{0,1:T(8,128)(2,1)S(1)} %copy.11, bf16[8,128,512]{1,2,0:T(8,128)(2,1)S(1)} %all-to-all-done, f32[128]{0:T(128)S(1)} %get-tuple-element.9, s32[4096]{0:T(1024)S(1)} %shift_right_arithmetic.23, s32[128,128]{0,1:T(8,128)S(1)} %copy.12, f32[4096]{0:T(1024)S(1)} %copy-done.1), kind=kLoop, calls=%fused_computation.9 | loop fusion | flops 6287232 | bytes 2212864 | tf_op jit(solution)/shard_map/reduce_sum | solution.py:26
  25.6 1.4 %fusion.6 = bf16[128,4096]{0,1:T(8,128)(2,1)S(1)} fusion(bf16[128,4096]{0,1:T(8,128)(2,1)S(1)} %copy.11, bf16[8,128,512]{1,2,0:T(8,128)(2,1)S(1)} %all-to-all-done, f32[128]{0:T(128)S(1)} %broadcast_multiply_fusion.2, f32[128]{0:T(128)S(1)} %get-tuple-element.9, f32[4096]{0:T(1024)S(1)} %copy-done.1, f32[128]{0:T(128)S(1)} %get-tuple-element.8, ...), kind=kLoop, calls=%fused_computation.8 | loop fusion | flops 7340032 | bytes 3245568 | tf_op jit(solution)/shard_map/convert_element_type | solution.py:25
  27.1 1.3 %copy.14 = bf16[128,4096]{1,0:T(8,128)(2,1)} copy(bf16[128,4096]{0,1:T(8,128)(2,1)S(1)} %fusion.6) | data formatting | bytes 2097152
  28.4 22.3 %all-reduce = f32[4096]{0:T(1024)S(1)} all-reduce(f32[4096]{0:T(1024)S(1)} %get-tuple-element.6), channel_id=2, replica_groups=mesh['aa'=4,'ba'=8] {'ba'}, use_global_device_ids=true, to_apply=%region_3.0.clone | all-reduce | flops 4096 | bytes 32768
  50.7 0.1 dynamic-slice.1
  50.8 11.9 %psum.7 = f32[512]{0:T(512)S(1)} all-reduce(f32[512]{0:T(512)S(1)} %dynamic-slice.1), channel_id=1, replica_groups=mesh['aa'=4,'ba'=8] {'aa'}, use_global_device_ids=true, to_apply=%region_4.0 | all-reduce | flops 512 | bytes 4096 | tf_op jit(solution)/shard_map/psum | solution.py:39
  62.7 0.6 broadcast_multiply_fusion
  (3 shorter events, 0.0 us)
Async XLA Ops:
  2.9 5.3 %copy-start = (bf16[128,4096]{1,0:T(8,128)(2,1)S(1)}, bf16[128,4096]{1,0:T(8,128)(2,1)}, u32[]{:S(2)}) copy-start(bf16[128,4096]{1,0:T(8,128)(2,1)} %param.5) | copy-start | bytes 3145732
  2.9 20.7 %all-to-all-start = ((bf16[8,128,512]{1,2,0:T(8,128)(2,1)}), bf16[8,128,512]{1,2,0:T(8,128)(2,1)S(1)}, u32[]{:S(2)}, u32[]{:S(2)}) async-start(bf16[8,128,512]{1,2,0:T(8,128)(2,1)} %copy.13), calls=%async_computation | async-start | bytes 2097152 | tf_op jit(solution)/shard_map/all_to_all | solution.py:34
  8.2 0.8 %copy-start.2 = (s32[128,128]{1,0:T(8,128)S(1)}, s32[128,128]{1,0:T(8,128)}, u32[]{:S(2)}) copy-start(s32[128,128]{1,0:T(8,128)} %param.6) | copy-start | bytes 196612
  8.2 0.9 %copy-start.3 = (u32[32]{0:T(128)S(1)}, u32[32]{0:T(128)}, u32[]{:S(2)}) copy-start(u32[32]{0:T(128)} %constant.16) | copy-start | bytes 388
  8.9 14.7 %copy-start.1 = (f32[4096]{0:T(1024)S(1)}, f32[4096]{0:T(1024)}, u32[]{:S(2)}) copy-start(f32[4096]{0:T(1024)} %param.7) | copy-start | bytes 49156
where the time goes:
time: 63.6 us; the launch traced here: 63.3 us
  blocking collectives  34.2 us (54%)
  waiting for transfers between devices  12.4 us (19%)
  starting transfers between devices  5.33 us (8%)
  local copies, waits for them, and re-layouts  5.13 us (8%)
  other arithmetic  4.78 us (8%)
  between operations  1.38 us (2%)
    unnamed x1, blocking collectives  22.3 us
    all_to_all x1, waiting for transfers between devices, per_device(): lax.all_to_all(pieces, 'ba', split_axis=0, concat_axis=2, tiled=True)  12.4 us
    psum x1, blocking collectives, per_device(): share = lax.psum(owned, 'aa')  11.9 us
    all_to_all x1, starting transfers between devices, per_device(): lax.all_to_all(pieces, 'ba', split_axis=0, concat_axis=2, tiled=True)  5.33 us
    unnamed x13, local copies, waits for them, and re-layouts  2.78 us
    reshape x1, local copies, waits for them, and re-layouts, per_device(): pieces = grad_out.reshape(groups, rows, grad_out.shape[1])  2.26 us
    reduce_sum x1, other arithmetic, rows_backward(): partial_sum = jnp.sum(grads * normed, axis=0)  2.02 us
    convert_element_type x1, other arithmetic, rows_backward(): (inverse * (scaled - normed * centre) * keep * (1.0 / KEEP_RATE)).astype(...  1.43 us
  transfers between devices with their start and end apart: 1, of which 1 were waited for; matrix products, arithmetic and copies ran while one was open for 3% of the time, Pallas kernels for 0%

commit v1 on v0

--- a/solution.py
+++ b/solution.py
@@ -31,7 +31,10 @@
     groups = lax.axis_size("ba")
     rows = grad_out.shape[0] // groups
     pieces = grad_out.reshape(groups, rows, grad_out.shape[1])
-    arrived = lax.all_to_all(pieces, "ba", split_axis=0, concat_axis=2, tiled=True)
+    arrived = jnp.concatenate(
+        lax.all_to_all(jnp.stack(jnp.split(pieces, lax.axis_size("ba"), axis=0)), "ba", 0, 0),
+        axis=2,
+    )
     grad_rows = arrived.reshape(rows, arrived.shape[2])
     grad_in, partial_sum = rows_backward(grad_rows, saved_input, keep_bits, gain)
     total_tokens = rows * groups * lax.axis_size("aa")

time: 63.6 us -> 80 us (1.26)
  local copies, waits for them, and re-layouts: 5.13 us -> 18.3 us
  other arithmetic: 4.78 us -> 7.74 us
    unnamed x13 -> x20, local copies, waits for them, and re-layouts: 2.78 us -> 14.7 us
    reshape x1 -> x0, local copies, waits for them, and re-layouts: 2.26 us -> none  [per_device(): pieces = grad_out.reshape(groups, rows, grad_out.shape[1])]
    convert_element_type x0 -> x1, local copies, waits for them, and re-layouts: none -> 1.92 us  [rows_backward(): grads = grad_rows.astype(jnp.float32)]
    convert_element_type x0 -> x1, other arithmetic: none -> 1.64 us  [rows_backward(): grads = grad_rows.astype(jnp.float32)]
    another operation x0 -> x1, local copies, waits for them, and re-layouts: none -> 1.57 us  [per_device(): jnp.stack(jnp.split(pieces, lax.axis_size('ba'), axis=0))]
    convert_element_type x1, other arithmetic: 1.43 us -> 2.59 us  [rows_backward(): (inverse * (scaled - normed * centre) * keep * (1.0 / KEEP_RATE)).astype(...]
where the time goes in v1:
time: 80 us; the launch traced here: 79.5 us
  blocking collectives  34.2 us (43%)
  local copies, waits for them, and re-layouts  18.3 us (23%)
  waiting for transfers between devices  12.5 us (16%)
  other arithmetic  7.74 us (10%)
  starting transfers between devices  5.33 us (7%)
  between operations  1.39 us (2%)
    unnamed x1, blocking collectives  22.3 us
    unnamed x20, local copies, waits for them, and re-layouts  14.7 us
    all_to_all x1, waiting for transfers between devices, per_device(): lax.all_to_all(jnp.stack(jnp.split(pieces, lax.axis_size('ba'), axis=0)),...  12.5 us
    psum x1, blocking collectives, per_device(): share = lax.psum(owned, 'aa')  11.9 us
    all_to_all x1, starting transfers between devices, per_device(): lax.all_to_all(jnp.stack(jnp.split(pieces, lax.axis_size('ba'), axis=0)),...  5.33 us
    convert_element_type x1, other arithmetic, rows_backward(): (inverse * (scaled - normed * centre) * keep * (1.0 / KEEP_RATE)).astype(...  2.59 us
    reduce_sum x1, other arithmetic, rows_backward(): partial_sum = jnp.sum(grads * normed, axis=0)  2.2 us
    convert_element_type x1, local copies, waits for them, and re-layouts, rows_backward(): grads = grad_rows.astype(jnp.float32)  1.92 us
  transfers between devices with their start and end apart: 1, of which 1 were waited for; matrix products, arithmetic and copies ran while one was open for 3% of the time, Pallas kernels for 0%

profile of v1, /device:TPU:0, one launch (start us, length us, event | category | flops | bytes accessed | tf_op | source)
XLA Modules:
  0.0 79.5 jit_solution(14299120545742476879)
XLA Ops:
  0.6 0.0 copy-start
  0.6 1.7 %bitcast_dynamic-update-slice_fusion.7 = bf16[8,1,128,512]{3,2,1,0:T(8,128)(2,1)} fusion(bf16[1024,512]{1,0:T(8,128)(2,1)} %param.4), kind=kLoop, calls=%fused_computation.21 | loop fusion | bytes 262144
  2.3 1.6 %bitcast_dynamic-update-slice_fusion.6 = bf16[8,1,128,512]{3,2,1,0:T(8,128)(2,1)} fusion(bf16[8,1,128,512]{3,2,1,0:T(8,128)(2,1)} %bitcast_dynamic-update-slice_fusion.7, bf16[1024,512]{1,0:T(8,128)(2,1)} %param.4), kind=kLoop, calls=%fused_computation.20 | loop fusion | bytes 262144
  3.9 1.6 %bitcast_dynamic-update-slice_fusion.5 = bf16[8,1,128,512]{3,2,1,0:T(8,128)(2,1)} fusion(bf16[8,1,128,512]{3,2,1,0:T(8,128)(2,1)} %bitcast_dynamic-update-slice_fusion.6, bf16[1024,512]{1,0:T(8,128)(2,1)} %param.4), kind=kLoop, calls=%fused_computation.19 | loop fusion | bytes 262144
  5.4 1.6 %bitcast_dynamic-update-slice_fusion.4 = bf16[8,1,128,512]{3,2,1,0:T(8,128)(2,1)} fusion(bf16[8,1,128,512]{3,2,1,0:T(8,128)(2,1)} %bitcast_dynamic-update-slice_fusion.5, bf16[1024,512]{1,0:T(8,128)(2,1)} %param.4), kind=kLoop, calls=%fused_computation.18 | loop fusion | bytes 262144
  7.0 1.6 %bitcast_dynamic-update-slice_fusion.3 = bf16[8,1,128,512]{3,2,1,0:T(8,128)(2,1)} fusion(bf16[8,1,128,512]{3,2,1,0:T(8,128)(2,1)} %bitcast_dynamic-update-slice_fusion.4, bf16[1024,512]{1,0:T(8,128)(2,1)} %param.4), kind=kLoop, calls=%fused_computation.17 | loop fusion | bytes 262144
  8.6 1.6 %bitcast_dynamic-update-slice_fusion.2 = bf16[8,1,128,512]{3,2,1,0:T(8,128)(2,1)} fusion(bf16[8,1,128,512]{3,2,1,0:T(8,128)(2,1)} %bitcast_dynamic-update-slice_fusion.3, bf16[1024,512]{1,0:T(8,128)(2,1)} %param.4), kind=kLoop, calls=%fused_computation.16 | loop fusion | bytes 262144
  10.1 1.6 %bitcast_dynamic-update-slice_fusion.1 = bf16[8,1,128,512]{3,2,1,0:T(8,128)(2,1)} fusion(bf16[8,1,128,512]{3,2,1,0:T(8,128)(2,1)} %bitcast_dynamic-update-slice_fusion.2, bf16[1024,512]{1,0:T(8,128)(2,1)} %param.4), kind=kLoop, calls=%fused_computation.15 | loop fusion | bytes 262144
  11.7 1.6 %bitcast_dynamic-update-slice_fusion = bf16[8,1,128,512]{3,2,1,0:T(8,128)(2,1)} fusion(bf16[8,1,128,512]{3,2,1,0:T(8,128)(2,1)} %bitcast_dynamic-update-slice_fusion.1, bf16[1024,512]{1,0:T(8,128)(2,1)} %param.4), kind=kLoop, calls=%fused_computation.14 | loop fusion | bytes 262144 | tf_op jit(solution)/shard_map/stack | solution.py:35
  13.3 0.0 copy-start.2
  13.3 0.0 copy-start.3
  13.3 5.3 %all-to-all-start = ((bf16[8,1,128,512]{3,2,1,0:T(8,128)(2,1)}), bf16[8,1,128,512]{3,2,1,0:T(8,128)(2,1)S(1)}, u32[]{:S(2)}, u32[]{:S(2)}) async-start(bf16[8,1,128,512]{3,2,1,0:T(8,128)(2,1)} %bitcast_dynamic-update-slice_fusion), calls=%async_computation | async-start | bytes 2097152 | tf_op jit(solution)/shard_map/all_to_all | solution.py:35
  18.6 0.0 copy-done
  18.6 0.7 copy.11
  19.3 0.1 shift_right_arithmetic.23
  19.4 0.0 copy-done.2
  19.4 0.1 copy.12
  19.5 0.0 copy-done.3
  19.5 0.6 dynamic-slice
  20.7 0.7 multiply_reduce_fusion.1
  21.5 12.5 %all-to-all-done = bf16[8,1,128,512]{3,2,1,0:T(8,128)(2,1)S(1)} async-done(((bf16[8,1,128,512]{3,2,1,0:T(8,128)(2,1)}), bf16[8,1,128,512]{3,2,1,0:T(8,128)(2,1)S(1)}, u32[]{:S(2)}, u32[]{:S(2)}) %all-to-all-start) | async-done | bytes 1048608 | tf_op jit(solution)/shard_map/all_to_all | solution.py:35
  34.0 1.6 %convert_bitcast_fusion = f32[1,128,8,512]{3,1,0,2:T(8,128)} fusion(bf16[8,1,128,512]{3,2,1,0:T(8,128)(2,1)S(1)} %all-to-all-done), kind=kLoop, calls=%fused_computation.10 | loop fusion | flops 524288 | bytes 3145728 | tf_op jit(solution)/shard_map/convert_element_type | solution.py:22
  35.6 0.0 copy-start.1
  35.6 1.9 %copy.13 = f32[1,128,8,512]{1,3,2,0:T(8,128)S(1)} copy(f32[1,128,8,512]{3,1,0,2:T(8,128)} %convert_bitcast_fusion) | data formatting | bytes 4194304 | tf_op jit(solution)/shard_map/convert_element_type | solution.py:22
  37.5 0.0 copy-done.1
  37.6 2.2 %fusion = (f32[4096]{0:T(1024)S(1)}, f32[128]{0:T(128)S(1)}) fusion(f32[1,128,8,512]{1,3,2,0:T(8,128)S(1)} %copy.13, bf16[128,4096]{0,1:T(8,128)(2,1)S(1)} %copy.11, f32[128]{0:T(128)S(1)} %get-tuple-element.9, s32[4096]{0:T(1024)S(1)} %shift_right_arithmetic.23, s32[128,128]{0,1:T(8,128)S(1)} %copy.12, f32[4096]{0:T(1024)S(1)} %copy-done.1), kind=kLoop, calls=%fused_computation.2 | loop fusion | flops 5762944 | bytes 3261440 | tf_op jit(solution)/shard_map/reduce_sum | solution.py:26
  39.8 2.6 %fusion.6 = bf16[128,4096]{0,1:T(8,128)(2,1)} fusion(bf16[128,4096]{0,1:T(8,128)(2,1)S(1)} %copy.11, f32[1,128,8,512]{1,3,2,0:T(8,128)S(1)} %copy.13, f32[128]{0:T(128)S(1)} %broadcast_multiply_fusion.2, f32[128]{0:T(128)S(1)} %get-tuple-element.9, f32[4096]{0:T(1024)S(1)} %copy-done.1, f32[128]{0:T(128)S(1)} %get-tuple-element.8, ...), kind=kLoop, calls=%fused_computation.9 | loop fusion | flops 6815744 | bytes 4294144 | tf_op jit(solution)/shard_map/convert_element_type | solution.py:25
  42.4 2.3 %copy.14 = bf16[128,4096]{1,0:T(8,128)(2,1)} copy(bf16[128,4096]{0,1:T(8,128)(2,1)} %fusion.6) | data formatting | bytes 2097152
  44.6 22.3 %all-reduce = f32[4096]{0:T(1024)S(1)} all-reduce(f32[4096]{0:T(1024)S(1)} %get-tuple-element.6), channel_id=2, replica_groups=mesh['aa'=4,'ba'=8] {'ba'}, use_global_device_ids=true, to_apply=%region_3.0.clone | all-reduce | flops 4096 | bytes 32768
  66.9 0.1 dynamic-slice.1
  67.0 11.9 %psum.7 = f32[512]{0:T(512)S(1)} all-reduce(f32[512]{0:T(512)S(1)} %dynamic-slice.1), channel_id=1, replica_groups=mesh['aa'=4,'ba'=8] {'aa'}, use_global_device_ids=true, to_apply=%region_4.0 | all-reduce | flops 512 | bytes 4096 | tf_op jit(solution)/shard_map/psum | solution.py:42
  78.9 0.6 broadcast_multiply_fusion
  (3 shorter events, 0.0 us)
Async XLA Ops:
  0.6 18.0 %copy-start = (bf16[128,4096]{1,0:T(8,128)(2,1)S(1)}, bf16[128,4096]{1,0:T(8,128)(2,1)}, u32[]{:S(2)}) copy-start(bf16[128,4096]{1,0:T(8,128)(2,1)} %param.5) | copy-start | bytes 3145732
  13.3 6.1 %copy-start.2 = (s32[128,128]{1,0:T(8,128)S(1)}, s32[128,128]{1,0:T(8,128)}, u32[]{:S(2)}) copy-start(s32[128,128]{1,0:T(8,128)} %param.6) | copy-start | bytes 196612
  13.3 6.2 %copy-start.3 = (u32[32]{0:T(128)S(1)}, u32[32]{0:T(128)}, u32[]{:S(2)}) copy-start(u32[32]{0:T(128)} %constant.16) | copy-start | bytes 388
  13.3 20.7 %all-to-all-start = ((bf16[8,1,128,512]{3,2,1,0:T(8,128)(2,1)}), bf16[8,1,128,512]{3,2,1,0:T(8,128)(2,1)S(1)}, u32[]{:S(2)}, u32[]{:S(2)}) async-start(bf16[8,1,128,512]{3,2,1,0:T(8,128)(2,1)} %bitcast_dynamic-update-slice_fusion), calls=%async_computation | async-start | bytes 2097152 | tf_op jit(solution)/shard_map/all_to_all | solution.py:35
  35.6 1.9 %copy-start.1 = (f32[4096]{0:T(1024)S(1)}, f32[4096]{0:T(1024)}, u32[]{:S(2)}) copy-start(f32[4096]{0:T(1024)} %param.7) | copy-start | bytes 49156
